TPU v7x, 32 devices: a whole 2x2x4 slice. The times are simulated.
32 devices in a mesh: group: 2 (over x), expert: 16 (over z, y, core).
Axes of the slice: x: 2, y: 2, z: 4, core: 2. Of those that a mesh axis runs over, the one named last changes fastest.
Arguments:
- query: bfloat16 [32, 2048], P(('group', 'expert')), parts along dimension 0, may hold values from -600 to 600
- key_new: bfloat16 [32, 2048], P(('group', 'expert')), parts along dimension 0, may hold values from -6 to 6
- value_new: bfloat16 [32, 2048], P(('group', 'expert')), parts along dimension 0, may hold values from -6 to 6
- key_cache: bfloat16 [32, 256, 2048], P(('group', 'expert')), parts along dimension 0, may hold values from -6 to 6
- value_cache: bfloat16 [32, 256, 2048], P(('group', 'expert')), parts along dimension 0, may hold values from -6 to 6
- lengths: int32 [32], P(('group', 'expert')), parts along dimension 0, may hold values from 1 to 256
- hidden: bfloat16 [32, 2048], P(('group', 'expert')), parts along dimension 0, may hold values from -6 to 6
- routes: int32 [32], P('group'), parts along dimension 0, may hold values from 0 to 31, as said below
- w_out: bfloat16 [2048, 2048], P(None, 'expert'), may hold values from -0.125 to 0.125
- ln_gain: bfloat16 [2048], replicated, may hold values from 0.099609375 to 1.8984375
- router: bfloat16 [2048, 32], replicated, may hold values from -0.125 to 0.125
- shared_up: bfloat16 [2048, 8192], P(None, 'expert'), may hold values from -0.125 to 0.125
- shared_down: bfloat16 [8192, 2048], P('expert'), may hold values from -0.0625 to 0.0625
- expert_up: bfloat16 [2048, 131072], P(None, 'expert'), may hold values from -0.125 to 0.125
- expert_down: bfloat16 [131072, 2048], P('expert'), may hold values from -0.09375 to 0.09375
Outputs:
- layer_out: bfloat16 [32, 2048], P(('group', 'expert')), parts along dimension 0
There are 2 independent parts, one for each index of `group`. A program takes and returns all parts, laid end to end along the dimension named above; an argument that names none is the same for every part. Nothing has to cross between parts.
Inputs may be any that keep to these rules, and one draw needn't show every extreme that they name: `routes`: no expert is named by more than 2 tokens of the group, and in every draw some expert is named by exactly 2.
All inputs are finite; a program needn't handle non-finite values.
Results may differ from a plain program's by a relative error of at most 0.0085.
Values may be sent and summed in bfloat16 or wider, within the bound.
No kernel may reach another device: no remote copies, remote signals or barrier semaphores. Data moves between devices by JAX's collectives and lax.ppermute only.
A program may use at most 128 MiB of HBM per device.

v0:
```python
import math
import jax
import jax.numpy as jnp
from jax import lax
from jax.sharding import PartitionSpec as P

D = 2048
HEADS = 16
HEAD_DIM = 128
FF = 4096
EXPERTS = 32


def attend(query, key_new, value_new, key_cache, value_cache, lengths):
    seq_count = query.shape[0]
    cache_len = key_cache.shape[1]
    scale_factor = 1.0 / math.sqrt(HEAD_DIM)
    head_query = query.reshape(seq_count, HEADS, HEAD_DIM)
    head_keys = key_cache.reshape(seq_count, cache_len, HEADS, HEAD_DIM)
    head_values = value_cache.reshape(seq_count, cache_len, HEADS, HEAD_DIM)
    scores = (
        jnp.einsum("shd,schd->shc", head_query, head_keys, preferred_element_type=jnp.float32)
        * scale_factor
    )
    own_score = (
        jnp.einsum(
            "shd,shd->sh",
            head_query,
            key_new.reshape(seq_count, HEADS, HEAD_DIM),
            preferred_element_type=jnp.float32,
        )
        * scale_factor
    )
    positions = jnp.arange(cache_len, dtype=jnp.int32)
    scores = jnp.where(positions[None, None, :] < lengths[:, None, None], scores, -1e30)
    top_score = jnp.maximum(jnp.max(scores, axis=2), own_score)
    weights = jnp.exp(scores - top_score[:, :, None])
    own_weight = jnp.exp(own_score - top_score)
    normalizer = jnp.sum(weights, axis=2) + own_weight
    weights = (weights / normalizer[:, :, None]).astype(jnp.bfloat16)
    own_weight = (own_weight / normalizer).astype(jnp.bfloat16)
    mixed_values = jnp.einsum(
        "shc,schd->shd", weights, head_values, preferred_element_type=jnp.float32
    )
    mixed_values = mixed_values + own_weight.astype(jnp.float32)[:, :, None] * value_new.reshape(
        seq_count, HEADS, HEAD_DIM
    ).astype(jnp.float32)
    return mixed_values.reshape(seq_count, HEADS * HEAD_DIM).astype(jnp.bfloat16)


def body(
    query,
    key_new,
    value_new,
    key_cache,
    value_cache,
    lengths,
    hidden,
    routes,
    w_out,
    ln_gain,
    router,
    shared_up,
    shared_down,
    expert_up,
    expert_down,
):
    seq_count = query.shape[0]
    attended = attend(query, key_new, value_new, key_cache, value_cache, lengths)
    every_attended, every_hidden = (
        lax.all_gather(attended, "expert", axis=0, tiled=True),
        lax.all_gather(hidden, "expert", axis=0, tiled=True),
    )
    projected = jnp.dot(every_attended, w_out, preferred_element_type=jnp.float32).astype(
        jnp.bfloat16
    )
    every_projected = lax.all_gather(projected, "expert", axis=1, tiled=True)
    residual = every_hidden.astype(jnp.float32) + every_projected.astype(jnp.float32)
    centered = residual - jnp.mean(residual, axis=1, keepdims=True)
    variance = jnp.mean(centered * centered, axis=1, keepdims=True)
    normed = (
        centered / jnp.sqrt(jnp.maximum(variance, 0.25)) * ln_gain.astype(jnp.float32)
    ).astype(jnp.bfloat16)
    logits = jnp.dot(normed, router, preferred_element_type=jnp.float32)
    all_experts = jnp.arange(EXPERTS, dtype=jnp.int32)
    chosen = jnp.sum(jnp.where(routes[:, None] == all_experts[None, :], logits, 0.0), axis=1)
    gate_value = jax.nn.sigmoid(chosen)
    shared_hidden = jax.nn.gelu(
        jnp.dot(normed, shared_up, preferred_element_type=jnp.float32), approximate=True
    ).astype(jnp.bfloat16)
    total_tokens = routes.shape[0]
    capacity = 4 * total_tokens // EXPERTS
    column_count = expert_up.shape[1]
    local_units = min(column_count, FF)
    local_experts = column_count // local_units
    device_index = lax.axis_index("expert")
    first_expert = device_index * column_count // FF
    expert_ids = first_expert + jnp.arange(local_experts, dtype=jnp.int32)
    member = routes[:, None] == expert_ids[None, :]
    slot_rank = jnp.cumsum(member.astype(jnp.int32), axis=0) - 1
    slot_ids = jnp.arange(capacity, dtype=jnp.int32)
    placed = member[:, :, None] & (slot_rank[:, :, None] == slot_ids[None, None, :])
    picked = jnp.einsum(
        "skc,sd->kcd", placed.astype(jnp.bfloat16), normed, preferred_element_type=jnp.float32
    ).astype(jnp.bfloat16)
    up_local = expert_up.reshape(D, local_experts, local_units)
    inner_act = jax.nn.gelu(
        jnp.einsum("kcd,dkf->kcf", picked, up_local, preferred_element_type=jnp.float32),
        approximate=True,
    ).astype(jnp.bfloat16)
    down_local = expert_down.reshape(local_experts, local_units, D)
    result = jnp.einsum("kcf,kfd->kcd", inner_act, down_local, preferred_element_type=jnp.float32)
    spread = placed.astype(jnp.float32) * gate_value[:, None, None]
    summed = lax.psum_scatter(
        jnp.dot(shared_hidden, shared_down, preferred_element_type=jnp.float32)
        + jnp.einsum("skc,kcd->sd", spread, result, precision=lax.Precision.HIGHEST),
        "expert",
        scatter_dimension=0,
        tiled=True,
    )
    own_residual = lax.dynamic_slice_in_dim(residual, device_index * seq_count, seq_count, 0)
    combined = own_residual + summed
    return combined.astype(jnp.bfloat16)


def solution(mesh):
    placed = (
        P(("group", "expert"), None),
        P(("group", "expert"), None),
        P(("group", "expert"), None),
        P(("group", "expert"), None, None),
        P(("group", "expert"), None, None),
        P(("group", "expert")),
        P(("group", "expert"), None),
        P("group"),
        P(None, "expert"),
        P(),
        P(),
        P(None, "expert"),
        P("expert", None),
        P(None, "expert"),
        P("expert", None),
    )
    return jax.shard_map(
        body, mesh=mesh, in_specs=placed, out_specs=P(("group", "expert"), None), check_vma=False
    )
```

profile of v0, /device:TPU:8, one launch (start us, length us, event | category | flops | bytes accessed | tf_op | source)
XLA Modules:
  0.0 203.4 jit_solution(5360927554412156418)
XLA Ops:
  6.5 1.6 copy.43
  8.8 0.9 fusion.42
  9.8 0.7 reduce.5
  10.5 0.7 reduce.6
  11.2 0.1 fusion.39
  11.4 0.1 fusion.41
  11.5 0.2 fusion.38
  11.7 0.1 fusion.44
  11.8 1.5 copy.47
  13.2 0.7 convert_element_type.86
  13.9 0.3 fusion.4
  14.3 0.1 add_convert_fusion
  14.4 19.2 %all-gather.1 = bf16[16,1,2048]{2,1,0:T(2,128)(2,1)S(1)} all-gather(bf16[1,1,2048]{2,1,0:T(2,128)(2,1)S(1)} %reshape.187), channel_id=1, replica_groups=mesh['group'=2,'expert'=16] {'expert'}, dimensions={0}, use_global_device_ids=true | all-gather | bytes 69632 | tf_op jit(solution)/shard_map/all_gather | solution.py:71
  33.5 1.2 convolution_convert_fusion.1
  34.8 17.6 %all_gather.11 = bf16[16,2048]{1,0:T(8,128)(2,1)S(1)} all-gather(bf16[16,128]{1,0:T(8,128)(2,1)S(1)} %convolution_convert_fusion.1), channel_id=1, replica_groups=mesh['group'=2,'expert'=16] {'expert'}, dimensions={1}, use_global_device_ids=true | all-gather | bytes 69632 | tf_op jit(solution)/shard_map/all_gather | solution.py:77
  52.4 19.3 %all-gather = bf16[16,1,2048]{2,1,0:T(2,128)(2,1)S(1)} all-gather(bf16[1,1,2048]{2,1,0:T(2,128)(2,1)} %bitcast.69), channel_id=1, replica_groups=mesh['group'=2,'expert'=16] {'expert'}, dimensions={0}, use_global_device_ids=true | all-gather | bytes 69632 | tf_op jit(solution)/shard_map/all_gather | solution.py:72
  71.7 0.2 fusion.57
  71.9 0.2 multiply_reduce_fusion
  72.1 0.7 convert_element_type.79
  72.8 0.7 fusion.56
  73.6 0.1 copy.30
  73.7 0.1 copy.29
  73.8 0.1 multiply_convert_fusion
  73.8 1.2 fusion.3
  75.0 12.2 %fusion.15 = bf16[2,2,4096]{2,1,0:T(2,128)(2,1)S(1)} fusion(bf16[256,2,8,4096]{3,2,1,0:T(8,128)(2,1)} %bitcast.63, bf16[16,2048]{1,0:T(8,128)(2,1)S(1)} %multiply_convert_fusion, pred[16,2,2]{0,1,2:T(4,128)(4,1)S(1)} %compare_and_fusion), kind=kOutput, calls=%fused_computation.22 | convolution fusion | flops 67526656 | bytes 33652800 | tf_op jit(solution)/shard_map/kcd,dkf->kcf/dot_general | solution.py:108
  87.3 12.8 %fusion.60 = f32[2,2,2048]{2,1,0:T(2,128)S(1)} fusion(bf16[2,2,4096]{2,1,0:T(2,128)(2,1)S(1)} %fusion.15, bf16[2,4096,2048]{2,1,0:T(8,128)(2,1)} %bitcast.64), kind=kOutput, calls=%fused_computation.80 | convolution fusion | flops 67108864 | bytes 33619968 | tf_op jit(solution)/shard_map/kcf,kfd->kcd/dot_general | solution.py:112
  100.1 0.4 convolution_bitcast_fusion
  100.5 3.0 %convolution_add_fusion = f32[16,2048]{1,0:T(8,128)} fusion(f32[16,2048]{1,0:T(8,128)S(1)} %convolution_bitcast_fusion, bf16[512,2048]{1,0:T(8,128)(2,1)S(1)} %copy-done, bf16[16,2048]{1,0:T(8,128)(2,1)S(1)} %multiply_convert_fusion, bf16[2048,512]{1,0:T(8,128)(2,1)} %param.26), kind=kOutput, calls=%fused_computation.4 | convolution fusion | flops 67215360 | bytes 4521984 | tf_op jit(solution)/shard_map/dot_general | solution.py:115
  103.5 0.0 all-reduce.3.cloned.1.call-update
  103.5 0.6 dynamic-slice
  104.2 90.3 %all-reduce.3.cloned.1.call-done = f32[16,2048]{1,0:T(8,128)} async-done(((f32[16,2048]{1,0:T(8,128)}), f32[16,2048]{1,0:T(8,128)}) %all-reduce.3.cloned.1.call-update) | async-done | bytes 131088
  194.5 2.1 %fusion.40 = bf16[1,2048]{1,0:T(2,128)(2,1)} fusion(f32[16,2048]{1,0:T(8,128)} %all-reduce.3.cloned.1.call-done, u32[]{:T(128)} %bitcast.14, f32[16,2048]{1,0:T(8,128)S(1)} %get-tuple-element.6, s32[]{:T(128)S(6)} %select_n.18), kind=kLoop, calls=%fused_computation.48 | loop fusion | flops 4096 | bytes 20488 | tf_op jit(solution)/shard_map/convert_element_type | solution.py:123
  (16 shorter events, 0.1 us)
Async XLA Ops:
  6.5 93.9 %copy-start = (bf16[512,2048]{1,0:T(8,128)(2,1)S(1)}, bf16[512,2048]{1,0:T(8,128)(2,1)}, u32[]{:S(2)}) copy-start(bf16[512,2048]{1,0:T(8,128)(2,1)} %param.27) | copy-start | bytes 6291460
  6.5 187.9 %all-reduce.3.cloned.1.call-start = ((), (), s32[]{:S(2)}) async-start(), calls=%async_computation | async-start | bytes 262144
  87.2 16.3 %copy-start.1 = (u32[32]{0:T(128)S(1)}, u32[32]{0:T(128)}, u32[]{:S(2)}) copy-start(u32[32]{0:T(128)} %constant.69) | copy-start | bytes 388
Sparse Core Ops, SparseCore 0:
  103.6 90.8 all-reduce.2
where the time goes:
time: 204 us; the launch traced here: 203 us
  waiting for transfers between devices  90.3 us (44%)
  blocking collectives  56.1 us (28%)
  matrix products  32 us (16%)
  between operations  14.2 us (7%)
  other arithmetic  6.8 us (3%)
  local copies, waits for them, and re-layouts  3.92 us (2%)
    unnamed x2, waiting for transfers between devices  90.3 us
    all_gather x1, blocking collectives, body(): lax.all_gather(hidden, 'expert', axis=0, tiled=True)  19.3 us
    all_gather x1, blocking collectives, body(): lax.all_gather(attended, 'expert', axis=0, tiled=True)  19.2 us
    all_gather x1, blocking collectives, body(): every_projected = lax.all_gather(projected, 'expert', axis=1, tiled=True)  17.6 us
    dot_general x1, matrix products, body(): jnp.einsum('kcf,kfd->kcd', inner_act, down_local, preferred_element_type=...  12.8 us
    dot_general x1, matrix products, body(): jnp.einsum('kcd,dkf->kcf', picked, up_local, preferred_element_type=jnp.f...  12.2 us
  transfers between devices with their start and end apart: 1, of which 1 were waited for; matrix products, arithmetic and copies ran while one was open for 0% of the time, Pallas kernels for 0%

commit v1 on v0

--- a/solution.py
+++ b/solution.py
@@ -69,7 +69,9 @@
     attended = attend(query, key_new, value_new, key_cache, value_cache, lengths)
     every_attended, every_hidden = (
         lax.all_gather(attended, "expert", axis=0, tiled=True),
-        lax.all_gather(hidden, "expert", axis=0, tiled=True),
+        jnp.concatenate(
+            lax.all_to_all(jnp.stack([hidden] * lax.axis_size("expert")), "expert", 0, 0), axis=0
+        ),
     )
     projected = jnp.dot(every_attended, w_out, preferred_element_type=jnp.float32).astype(
         jnp.bfloat16

time: 204 us -> 195 us (0.956)
  blocking collectives: 56.1 us -> 36.5 us
  starting transfers between devices: 0.01 us -> 6.33 us
    all_gather x1 -> x0, blocking collectives: 19.3 us -> none  [body(): lax.all_gather(hidden, 'expert', axis=0, tiled=True)]
    all_to_all x0 -> x1, starting transfers between devices: none -> 6.3 us  [body(): lax.all_to_all(jnp.stack([hidden] * lax.axis_size('expert')), 'expert', 0...]
  transfers between devices with their start and end apart: 1 -> 2, of which waited for: 1 -> 1; matrix products, arithmetic and copies ran while one was open for 0% -> 5% of each run, Pallas kernels for 0% -> 0%
where the time goes in v1:
time: 195 us; the launch traced here: 194 us
  waiting for transfers between devices  91.5 us (47%)
  blocking collectives  36.5 us (19%)
  matrix products  32 us (16%)
  between operations  14.2 us (7%)
  other arithmetic  8.67 us (4%)
  starting transfers between devices  6.33 us (3%)
  local copies, waits for them, and re-layouts  5.07 us (3%)
    unnamed x2, waiting for transfers between devices  91.5 us
    all_gather x1, blocking collectives, body(): lax.all_gather(attended, 'expert', axis=0, tiled=True)  18.9 us
    all_gather x1, blocking collectives, body(): every_projected = lax.all_gather(projected, 'expert', axis=1, tiled=True)  17.6 us
    dot_general x1, matrix products, body(): jnp.einsum('kcf,kfd->kcd', inner_act, down_local, preferred_element_type=...  12.8 us
    dot_general x1, matrix products, body(): jnp.einsum('kcd,dkf->kcf', picked, up_local, preferred_element_type=jnp.f...  12.2 us
    all_to_all x1, starting transfers between devices, body(): lax.all_to_all(jnp.stack([hidden] * lax.axis_size('expert')), 'expert', 0...  6.3 us
  transfers between devices with their start and end apart: 2, of which 1 were waited for; matrix products, arithmetic and copies ran while one was open for 5% of the time, Pallas kernels for 0%

profile of v1, /device:TPU:8, one launch (start us, length us, event | category | flops | bytes accessed | tf_op | source)
XLA Modules:
  0.0 194.3 jit_solution(66056128570978143)
XLA Ops:
  6.5 0.9 reduce.5
  7.5 0.5 broadcast.144
  8.0 1.0 reduce.9
  9.0 0.7 reshape.208
  9.7 6.3 %all-to-all-start = ((bf16[16,2,1024]{2,1,0:T(2,128)(2,1)}), bf16[16,2,1024]{2,1,0:T(2,128)(2,1)S(1)}, u32[]{:S(2)}, u32[]{:S(2)}) async-start(bf16[16,2,1024]{2,1,0:T(2,128)(2,1)} %reshape.208), calls=%async_computation | async-start | bytes 131072 | tf_op jit(solution)/shard_map/all_to_all | solution.py:73
  16.0 1.5 copy.43
  17.5 0.7 reduce.6
  18.2 0.9 fusion.42
  19.8 0.7 reduce.7
  20.6 0.1 fusion.39
  20.7 0.1 fusion.41
  20.8 0.2 fusion.38
  21.1 1.5 copy.47
  22.6 0.7 convert_element_type.91
  23.3 0.3 fusion.4
  23.7 18.9 %all-gather = bf16[16,1,2048]{2,1,0:T(2,128)(2,1)S(1)} all-gather(bf16[1,1,2048]{2,1,0:T(2,128)(2,1)S(1)} %reshape.192), channel_id=1, replica_groups=mesh['group'=2,'expert'=16] {'expert'}, dimensions={0}, use_global_device_ids=true | all-gather | bytes 69632 | tf_op jit(solution)/shard_map/all_gather | solution.py:71
  42.6 0.7 fusion.56
  43.5 0.1 copy.29
  43.5 1.2 convolution_convert_fusion.1
  44.8 0.7 convert_element_type.83
  45.5 17.6 %all_gather.7 = bf16[16,2048]{1,0:T(8,128)(2,1)S(1)} all-gather(bf16[16,128]{1,0:T(8,128)(2,1)S(1)} %convolution_convert_fusion.1), channel_id=1, replica_groups=mesh['group'=2,'expert'=16] {'expert'}, dimensions={1}, use_global_device_ids=true | all-gather | bytes 69632 | tf_op jit(solution)/shard_map/all_gather | solution.py:79
  63.1 0.2 fusion.57
  63.3 0.2 multiply_reduce_fusion
  63.5 0.1 multiply_convert_fusion
  63.6 1.2 fusion.3
  64.8 12.2 %fusion.15 = bf16[2,2,4096]{2,1,0:T(2,128)(2,1)S(1)} fusion(bf16[256,2,8,4096]{3,2,1,0:T(8,128)(2,1)} %bitcast.62, bf16[16,2048]{1,0:T(8,128)(2,1)S(1)} %multiply_convert_fusion, pred[16,2,2]{0,1,2:T(4,128)(4,1)S(1)} %compare_and_fusion), kind=kOutput, calls=%fused_computation.22 | convolution fusion | flops 67526656 | bytes 33652800 | tf_op jit(solution)/shard_map/kcd,dkf->kcf/dot_general | solution.py:110
  77.0 12.8 %fusion.60 = f32[2,2,2048]{2,1,0:T(2,128)S(1)} fusion(bf16[2,2,4096]{2,1,0:T(2,128)(2,1)S(1)} %fusion.15, bf16[2,4096,2048]{2,1,0:T(8,128)(2,1)} %bitcast.63), kind=kOutput, calls=%fused_computation.80 | convolution fusion | flops 67108864 | bytes 33619968 | tf_op jit(solution)/shard_map/kcf,kfd->kcd/dot_general | solution.py:114
  89.8 0.4 convolution_bitcast_fusion
  90.2 3.0 %convolution_add_fusion = f32[16,2048]{1,0:T(8,128)} fusion(f32[16,2048]{1,0:T(8,128)S(1)} %convolution_bitcast_fusion, bf16[512,2048]{1,0:T(8,128)(2,1)S(1)} %copy-done, bf16[16,2048]{1,0:T(8,128)(2,1)S(1)} %multiply_convert_fusion, bf16[2048,512]{1,0:T(8,128)(2,1)} %param.26), kind=kOutput, calls=%fused_computation.4 | convolution fusion | flops 67215360 | bytes 4521984 | tf_op jit(solution)/shard_map/dot_general | solution.py:117
  93.3 0.6 dynamic-slice
  93.9 91.4 %all-reduce.3.cloned.1.call-done = f32[16,2048]{1,0:T(8,128)} async-done(((f32[16,2048]{1,0:T(8,128)}), f32[16,2048]{1,0:T(8,128)}) %all-reduce.3.cloned.1.call-update) | async-done | bytes 131088
  185.4 2.1 %fusion.40 = bf16[1,2048]{1,0:T(2,128)(2,1)} fusion(f32[16,2048]{1,0:T(8,128)} %all-reduce.3.cloned.1.call-done, u32[]{:T(128)} %bitcast.13, f32[16,2048]{1,0:T(8,128)S(1)} %get-tuple-element.6, s32[]{:T(128)S(6)} %select_n.18), kind=kLoop, calls=%fused_computation.48 | loop fusion | flops 4096 | bytes 20488 | tf_op jit(solution)/shard_map/convert_element_type | solution.py:125
  (23 shorter events, 0.6 us)
Async XLA Ops:
  6.5 83.7 %copy-start = (bf16[512,2048]{1,0:T(8,128)(2,1)S(1)}, bf16[512,2048]{1,0:T(8,128)(2,1)}, u32[]{:S(2)}) copy-start(bf16[512,2048]{1,0:T(8,128)(2,1)} %param.27) | copy-start | bytes 6291460
  9.7 53.4 %all-to-all-start = ((bf16[16,2,1024]{2,1,0:T(2,128)(2,1)}), bf16[16,2,1024]{2,1,0:T(2,128)(2,1)S(1)}, u32[]{:S(2)}, u32[]{:S(2)}) async-start(bf16[16,2,1024]{2,1,0:T(2,128)(2,1)} %reshape.208), calls=%async_computation | async-start | bytes 131072 | tf_op jit(solution)/shard_map/all_to_all | solution.py:73
  16.0 169.4 %all-reduce.3.cloned.1.call-start = ((), (), s32[]{:S(2)}) async-start(), calls=%async_computation.1 | async-start | bytes 262144
  77.0 16.3 %copy-start.1 = (u32[32]{0:T(128)S(1)}, u32[32]{0:T(128)}, u32[]{:S(2)}) copy-start(u32[32]{0:T(128)} %constant.69) | copy-start | bytes 388
Sparse Core Ops, SparseCore 0:
  93.4 91.9 all-reduce.2
